TPU v7x, 256 devices: a whole 4x4x8 slice. The times are simulated.
256 devices in a mesh: seq: 4 (over x), batch: 64 (over z, y, core).
Axes of the slice: x: 4, y: 4, z: 8, core: 2. Of those that a mesh axis runs over, the one named last changes fastest.
Arguments:
- activations: bfloat16 [64, 3072, 4096], P('batch', 'seq'), may hold values from -48 to 48
- out_grads: bfloat16 [64, 3072, 4096], P('batch', 'seq'), may hold values from -0.875 to 0.875
- lengths: int32 [64, 3], P('batch'), may hold values from 1 to 1536, 3072 in all within a row
Outputs:
- act_factor: float32 [4096, 4096], P(('seq', 'batch'))
- grad_factor: float32 [4096, 4096], P(('seq', 'batch'))
Inputs may be any that keep to these rules, and one draw needn't show every extreme that they name: `lengths`: each row sums to 3072 and its largest entry is exactly 1536.
All inputs are finite; a program needn't handle non-finite values.
Results may differ from a plain program's by a relative error of at most 0.004.
Values may be sent and summed in bfloat16 or wider, within the bound.
A program may use at most 64 MiB of HBM per device.

v0:
```python
import jax
import jax.numpy as jnp
from jax import lax
from jax.sharding import PartitionSpec as P


def copy_for_each(value, axis):
    peers = lax.axis_size(axis)
    return lax.all_to_all(
        jnp.broadcast_to(value[None], (peers, *value.shape)), axis, 0, 0, tiled=True
    )


def of_everyone(value, axis):
    everything = copy_for_each(value, axis)
    return jnp.sum(everything, axis=0)


def together(arrays, axis):
    flat, at, gathered = (jnp.concatenate([a.reshape(-1) for a in arrays]), 0, [])
    subtotal = of_everyone(flat, axis)
    for a in arrays:
        gathered.append(subtotal[at : at + a.size].reshape(a.shape))
        at += a.size
    return tuple(gathered)


def sent_together(arrays, axis, dim, along):
    widths = [a.shape[along] for a in arrays]
    both = jnp.concatenate(arrays, axis=along)
    whole = lax.all_gather(both, axis, axis=dim, tiled=True)
    return tuple(jnp.split(whole, [sum(widths[:k]) for k in range(1, len(widths))], axis=along))


def local(activations, out_grads, lengths):
    act_local = activations[0]
    grad_local = out_grads[0]
    seq_lengths = lengths[0]
    tok_count = act_local.shape[0]
    width = act_local.shape[1]
    seq_count = seq_lengths.shape[0]
    group_size = lax.axis_size("seq")
    devices = group_size * lax.axis_size("batch")
    tile_rows = width // devices
    tile_start = lax.axis_index(("seq", "batch")) * tile_rows
    total_seqs = seq_count * lax.axis_size("batch")
    ends = jnp.cumsum(seq_lengths)
    starts = ends - seq_lengths
    position = lax.axis_index("seq") * tok_count + jnp.arange(tok_count, dtype=jnp.int32)
    member = (position[None, :] >= starts[:, None]) & (position[None, :] < ends[:, None])
    member = member.astype(jnp.bfloat16)
    act_part = jnp.dot(member, act_local, preferred_element_type=jnp.float32)
    grad_part = jnp.dot(member, grad_local, preferred_element_type=jnp.float32)
    act_sum, grad_sum = together((act_part, grad_part), "seq")
    act_rows = (act_sum / seq_lengths[:, None].astype(jnp.float32)).astype(jnp.bfloat16)
    grad_rows = grad_sum.astype(jnp.bfloat16)
    act_piece, grad_piece = sent_together((act_rows, grad_rows), "batch", 0, 1)
    act_cols = lax.dynamic_slice_in_dim(act_piece, tile_start, tile_rows, 1)
    grad_cols = lax.dynamic_slice_in_dim(grad_piece, tile_start, tile_rows, 1)
    dims = (((0,), (0,)), ((), ()))
    act_new = lax.dot_general(act_cols, act_piece, dims, preferred_element_type=jnp.float32)
    grad_new = lax.dot_general(grad_cols, grad_piece, dims, preferred_element_type=jnp.float32)
    return (act_new / total_seqs, grad_new / total_seqs)


def solution(mesh):
    in_specs = (P("batch", "seq", None), P("batch", "seq", None), P("batch", None))
    out_specs = (P(("seq", "batch"), None), P(("seq", "batch"), None))
    return jax.shard_map(local, mesh=mesh, in_specs=in_specs, out_specs=out_specs, check_vma=False)
```

profile of v0, /device:TPU:1, one launch (start us, length us, event | category | flops | bytes accessed | tf_op | source)
XLA Modules:
  0.0 127.8 jit_solution(1883959985801057864)
XLA Ops:
  7.2 0.8 reduce-window.7
  8.0 0.7 bitcast_subtract_fusion
  8.7 3.7 %fusion = f32[3,4096]{1,0:T(4,128)S(1)} fusion(bf16[1,768,4096]{2,1,0:T(8,128)(2,1)} %param.4, s32[768]{0:T(1024)S(1)} %iota_add_fusion, s32[3]{0:T(128)S(1)} %bitcast.16, s32[3]{0:T(128)S(1)} %bitcast_subtract_fusion), kind=kOutput, calls=%fused_computation | convolution fusion | flops 18881280 | bytes 6343704 | tf_op jit(solution)/shard_map/dot_general | solution.py:53
  12.5 3.7 %fusion.2 = f32[3,4096]{1,0:T(4,128)S(1)} fusion(bf16[1,768,4096]{2,1,0:T(8,128)(2,1)} %param.3, s32[768]{0:T(1024)S(1)} %iota_add_fusion, s32[3]{0:T(128)S(1)} %bitcast.17, s32[3]{0:T(128)S(1)} %bitcast_subtract_fusion), kind=kOutput, calls=%fused_computation.2 | convolution fusion | flops 18881280 | bytes 6343704 | tf_op jit(solution)/shard_map/dot_general | solution.py:52
  16.2 0.0 copy-start
  16.3 0.9 broadcast_in_dim.2
  17.2 4.8 %all-to-all-start = ((f32[4,1,24576]{2,1,0:T(1,128)}), f32[4,1,24576]{2,1,0:T(1,128)S(1)}, u32[]{:S(2)}, u32[]{:S(2)}) async-start(f32[4,1,24576]{2,1,0:T(1,128)} %broadcast_in_dim.2), calls=%async_computation | async-start | bytes 786432 | tf_op jit(solution)/shard_map/all_to_all | solution.py:9
  22.0 0.0 all-gather.3.cloned.1.call-start
  22.0 0.0 copy-done
  22.1 6.2 %all-to-all-done = f32[4,1,24576]{2,1,0:T(1,128)S(1)} async-done(((f32[4,1,24576]{2,1,0:T(1,128)}), f32[4,1,24576]{2,1,0:T(1,128)S(1)}, u32[]{:S(2)}, u32[]{:S(2)}) %all-to-all-start) | async-done | bytes 393248 | tf_op jit(solution)/shard_map/all_to_all | solution.py:9
  28.3 0.4 reduce_sum.9
  28.7 0.1 divide_convert_fusion
  28.8 0.7 maximum_bitcast_fusion
  29.5 0.0 all-gather.3.cloned.1.call-update
  29.5 83.0 %all-gather.3.cloned.1.call-done = bf16[64,3,8192]{2,1,0:T(4,128)(2,1)} async-done(((bf16[1,3,8192]{2,1,0:T(4,128)(2,1)}), bf16[64,3,8192]{2,1,0:T(4,128)(2,1)}) %all-gather.3.cloned.1.call-update) | async-done | bytes 3145744 | tf_op jit(solution)/shard_map/all_gather | solution.py:31
  112.5 6.0 %reshape.79 = bf16[192,8192]{1,0:T(8,128)(2,1)S(1)} reshape(bf16[64,3,8192]{2,1,0:T(4,128)(2,1)} %all-gather.3.cloned.1.call-done) | data formatting | bytes 6291456
  118.5 0.2 fusion.8
  118.7 1.1 convolution_multiply_fusion
  119.9 1.1 convolution_multiply_fusion.1
  (9 shorter events, 0.2 us)
Async XLA Ops:
  16.2 5.9 %copy-start = (s32[1,3]{1,0:T(1,128)S(1)}, s32[1,3]{1,0:T(1,128)}, u32[]{:S(2)}) copy-start(s32[1,3]{1,0:T(1,128)} %param.5) | copy-start | bytes 40
  17.2 11.1 %all-to-all-start = ((f32[4,1,24576]{2,1,0:T(1,128)}), f32[4,1,24576]{2,1,0:T(1,128)S(1)}, u32[]{:S(2)}, u32[]{:S(2)}) async-start(f32[4,1,24576]{2,1,0:T(1,128)} %broadcast_in_dim.2), calls=%async_computation | async-start | bytes 786432 | tf_op jit(solution)/shard_map/all_to_all | solution.py:9
  22.0 90.5 %all-gather.3.cloned.1.call-start = ((), (), s32[]{:S(2)}) async-start(), calls=%async_computation.1 | async-start | bytes 4259840 | tf_op jit(solution)/shard_map/all_gather | solution.py:31
Sparse Core Ops, SparseCore 0:
  29.6 82.8 all-gather.2
where the time goes:
time: 128 us
  waiting for transfers between devices  89.2 us (70%)
  between operations  14.1 us (11%)
  matrix products  9.75 us (8%)
  local copies, waits for them, and re-layouts  7.28 us (6%)
  starting transfers between devices  4.83 us (4%)
  other arithmetic  2.61 us (2%)
    all_gather x1, waiting for transfers between devices, sent_together(): whole = lax.all_gather(both, axis, axis=dim, tiled=True)  83 us
    all_to_all x1, waiting for transfers between devices, copy_for_each(): lax.all_to_all(jnp.broadcast_to(value[None], (peers, *value.shape)), axis...  6.23 us
    unnamed x3, local copies, waits for them, and re-layouts  5.99 us
    all_to_all x1, starting transfers between devices, copy_for_each(): lax.all_to_all(jnp.broadcast_to(value[None], (peers, *value.shape)), axis...  4.83 us
    dot_general x1, matrix products, local(): act_part = jnp.dot(member, act_local, preferred_element_type=jnp.float32)  3.74 us
    dot_general x1, matrix products, local(): grad_part = jnp.dot(member, grad_local, preferred_element_type=jnp.float32)  3.74 us
  transfers between devices with their start and end apart: 2, of which 2 were waited for; matrix products, arithmetic and copies ran while one was open for 0% of the time, Pallas kernels for 0%

commit v1 on v0

v1 whole, which is shorter than its diff:
```python
import jax
import jax.numpy as jnp
from jax import lax
from jax.experimental import pallas as pl
from jax.experimental.pallas import tpu as pltpu
from jax.sharding import PartitionSpec as P

NX, NY, NZ, NC = 4, 4, 8, 2
NB = NY * NC
LANES = 128
SEQS = 3
MESH = pl.DeviceIdType.MESH
F32, BF16 = jnp.float32, jnp.bfloat16


def kernel(
    act_hbm, grad_hbm, len_ref, out_ref,
    abuf, gbuf, parts, got, packed, rhs, lhs, tiles, landed,
    in_sem, s1_send, s1_recv, z_send, z_recv, x_send, x_recv, l_send, l_recv, o_send, o_recv,
):
    steps, tokens, wide = abuf.shape
    halves = steps // NX
    per_step = wide // LANES
    total_seqs = SEQS * NZ * NY * NC
    rows = LANES // NB
    chunk = 2 * SEQS * NB

    x = lax.axis_index("seq")
    b = lax.axis_index("batch")
    c = b % NC
    y = (b // NC) % NY
    z = b // (NC * NY)
    mine = y + NY * c
    g_me = y * NC + c

    def at(x_, y_, z_, c_):
        return (x_, (z_ * NY + y_) * NC + c_)

    def quarter(i):
        return (x + 1 + i // halves) % NX

    def loads(i):
        cols = pl.ds(pl.multiple_of(quarter(i) * (halves * wide) + (i % halves) * wide, wide), wide)
        return (
            pltpu.make_async_copy(act_hbm.at[0, :, cols], abuf.at[i], in_sem.at[0, i]),
            pltpu.make_async_copy(grad_hbm.at[0, :, cols], gbuf.at[i], in_sem.at[1, i]),
        )

    @pl.loop(0, steps)
    def _(i):
        for copy in loads(i):
            copy.start()

    barrier = pltpu.get_barrier_semaphore()

    def greet(target):
        pl.semaphore_signal(barrier, inc=1, device_id=target, device_id_type=MESH)

    @pl.loop(1, NX * NB)
    def _(k):
        other = (x * NB + g_me + k) % (NX * NB)
        greet(at(other // NB, (other % NB) // NC, z, other % NC))

    @pl.loop(1, NZ)
    def _(k):
        greet(at(x, y, (z + k) % NZ, c))

    src_y, src_c = z % NY, z // NY
    src_here = jnp.logical_and(src_y == y, src_c == c)

    @pl.loop(0, NZ)
    def _(k):
        @pl.when(jnp.logical_not(jnp.logical_and(src_here, k == z)))
        def _():
            greet(at(x, src_y, k, src_c))

    l0, l1, l2 = len_ref[0, 0], len_ref[0, 1], len_ref[0, 2]
    row = lax.broadcasted_iota(jnp.int32, (8, tokens), 0)
    pos = lax.broadcasted_iota(jnp.int32, (8, tokens), 1) + x * tokens

    def member(first):
        r = row - first
        start = jnp.where(r == 0, 0, jnp.where(r == 1, l0, l0 + l1))
        end = jnp.where(r == 0, l0, jnp.where(r == 1, l0 + l1, l0 + l1 + l2))
        inside = (r >= 0) & (r < SEQS) & (pos >= start) & (pos < end)
        return jnp.where(inside, 1.0, 0.0).astype(BF16)

    m_act, m_grad = member(0), member(SEQS)
    row_w = lax.broadcasted_iota(jnp.int32, (8, wide), 0)
    divisor = jnp.where(row_w == 0, l0, jnp.where(row_w == 1, l1, jnp.where(row_w == 2, l2, 1))).astype(F32)

    def s1_copy(slot_block, target, slot):
        return pltpu.make_async_remote_copy(
            src_ref=parts.at[slot_block], dst_ref=got.at[slot],
            send_sem=s1_send, recv_sem=s1_recv, device_id=target, device_id_type=MESH,
        )

    my_slot = x * NB + g_me
    home = x * NB + mine

    @pl.loop(0, steps)
    def _(i):
        for copy in loads(i):
            copy.wait()
        total = jnp.dot(m_act, abuf[i], preferred_element_type=F32)
        total += jnp.dot(m_grad, gbuf[i], preferred_element_type=F32)
        total = total / divisor
        q = quarter(i)
        first = q * NB + (i % halves) * per_step
        for j in range(per_step):
            parts[first + j] = total[:, j * LANES : (j + 1) * LANES]

        @pl.when(i == 0)
        def _():
            pl.semaphore_wait(barrier, NX * NB - 1 + NZ - 1 + NZ - jnp.where(mine == z, 1, 0))

        for j in range(per_step):
            zb = (i % halves) * per_step + j

            @pl.when(first + j != home)
            def _():
                s1_copy(first + j, at(q, zb % NY, z, zb // NY), my_slot).start()

    got[my_slot] = parts[home]
    pltpu.make_async_copy(got.at[pl.ds(0, NX * NB - 1)], got.at[pl.ds(0, NX * NB - 1)], s1_recv).wait()

    for g in range(NB):
        summed = got[g]
        for k in range(1, NX):
            summed += got[k * NB + g]
        packed[g * SEQS : (g + 1) * SEQS] = summed[0:SEQS]
        packed[SEQS * (NB + g) : SEQS * (NB + g + 1)] = summed[SEQS : 2 * SEQS]
    own = packed[...].astype(BF16)
    rhs[x, z] = own

    @pl.when(mine == z)
    def _():
        lhs[z] = own

    def z_copy(k):
        return pltpu.make_async_remote_copy(
            src_ref=rhs.at[x, z], dst_ref=rhs.at[x, z],
            send_sem=z_send, recv_sem=z_recv.at[z],
            device_id=at(x, y, (z + k) % NZ, c), device_id_type=MESH,
        )

    def x_copy(k, layer):
        return pltpu.make_async_remote_copy(
            src_ref=rhs.at[x, layer], dst_ref=rhs.at[x, layer],
            send_sem=x_send, recv_sem=x_recv.at[x],
            device_id=at((x + k) % NX, y, z, c), device_id_type=MESH,
        )

    def l_copy(d):
        return pltpu.make_async_remote_copy(
            src_ref=rhs.at[x, z], dst_ref=lhs.at[z],
            send_sem=l_send, recv_sem=l_recv.at[z],
            device_id=at(x, d // NC, mine, d % NC), device_id_type=MESH,
        )

    for k in (4, 3, 5, 2, 6, 1, 7):
        z_copy(k).start()
    for k in (2, 1, 3):
        x_copy(k, z).start()
    for k in range(NB):
        d = (g_me + 4 + k) % NB

        @pl.when(jnp.logical_not(jnp.logical_and(mine == z, d == g_me)))
        def _():
            l_copy(d).start()

    def arrived(ref, sem):
        pltpu.make_async_copy(ref, ref, sem).wait()

    for k in (1, 7, 2, 6, 3, 5, 4):
        layer = (z + k) % NZ
        arrived(rhs.at[x, layer], z_recv.at[layer])
        for kx in (2, 1, 3):
            x_copy(kx, layer).start()

    for k in range(NZ):
        @pl.when(jnp.logical_not(jnp.logical_and(src_here, k == z)))
        def _():
            arrived(lhs.at[k], l_recv.at[k])

    depth = NZ * chunk
    lcols = lhs[...].reshape(depth, LANES)
    in_act = lax.broadcasted_iota(jnp.int32, (depth, LANES), 0) % chunk < SEQS * NB
    act_only = jnp.where(in_act, 1.0, 0.0).astype(BF16)
    grad_only = jnp.where(in_act, 0.0, 1.0).astype(BF16)
    both = jnp.concatenate([lcols * act_only, lcols * grad_only], axis=1)

    for k in range(1, NX):
        who = (x + k) % NX
        arrived(rhs.at[who], x_recv.at[who])

    for k in range(NX):
        product = lax.dot_general(
            both, rhs[k].reshape(depth, LANES), (((0,), (0,)), ((), ())), preferred_element_type=F32
        )
        product = (product / total_seqs).astype(BF16)
        for d in range(NB):
            for kind in range(2):
                tiles[d, kind * rows : (kind + 1) * rows, k * LANES : (k + 1) * LANES] = product[
                    kind * LANES + d * rows : kind * LANES + (d + 1) * rows
                ]

    def o_copy(d):
        return pltpu.make_async_remote_copy(
            src_ref=tiles.at[d], dst_ref=landed.at[mine],
            send_sem=o_send, recv_sem=o_recv,
            device_id=at(x, d // NC, z, d % NC), device_id_type=MESH,
        )

    for k in (4, 5, 2, 3, 6, 7, 1):
        d = (g_me + k) % NB
        o_copy(d).start()
    landed[mine] = tiles[g_me]

    arrived(got.at[pl.ds(0, NX * NB - 1)], s1_send)
    arrived(rhs.at[0, pl.ds(0, NZ - 1)], z_send)
    arrived(rhs.at[pl.ds(0, NX - 1)], x_send)

    @pl.when(mine == z)
    def _():
        arrived(lhs.at[pl.ds(0, NB - 1)], l_send)

    @pl.when(mine != z)
    def _():
        arrived(lhs.at[pl.ds(0, NB)], l_send)

    arrived(landed.at[pl.ds(0, NB - 1)], o_recv)
    arrived(landed.at[pl.ds(0, NB - 1)], o_send)
    for q in range(NX):
        for zb in range(NB):
            cols = pl.ds((q * NB + zb) * LANES, LANES)
            for kind in range(2):
                out_ref[kind, :, cols] = landed[zb, kind * rows : (kind + 1) * rows, q * LANES : (q + 1) * LANES]


def local(activations, out_grads, lengths):
    tokens, width = activations.shape[1:]
    rows = width // (NX * NY * NZ * NC)
    steps = 2 * NX
    wide = width // steps
    chunk = 2 * SEQS * NB
    dma = pltpu.SemaphoreType.DMA
    out = pl.pallas_call(
        kernel,
        out_shape=jax.ShapeDtypeStruct((2, rows, width), BF16),
        in_specs=[
            pl.BlockSpec(memory_space=pl.ANY),
            pl.BlockSpec(memory_space=pl.ANY),
            pl.BlockSpec(memory_space=pltpu.SMEM),
        ],
        out_specs=pl.BlockSpec(memory_space=pltpu.VMEM),
        scratch_shapes=[
            pltpu.VMEM((steps, tokens, wide), BF16),
            pltpu.VMEM((steps, tokens, wide), BF16),
            pltpu.VMEM((NX * NB, 8, LANES), F32),
            pltpu.VMEM((NX * NB, 8, LANES), F32),
            pltpu.VMEM((chunk, LANES), F32),
            pltpu.VMEM((NX, NZ, chunk, LANES), BF16),
            pltpu.VMEM((NZ, chunk, LANES), BF16),
            pltpu.VMEM((NB, 2 * rows, NX * LANES), BF16),
            pltpu.VMEM((NB, 2 * rows, NX * LANES), BF16),
            dma((2, steps)),
            dma, dma,
            dma, dma((NZ,)),
            dma, dma((NX,)),
            dma, dma((NZ,)),
            dma, dma,
        ],
        compiler_params=pltpu.CompilerParams(collective_id=0, has_side_effects=True),
    )(activations, out_grads, lengths)
    wide_out = out.astype(F32)
    return wide_out[0], wide_out[1]


def solution(mesh):
    in_specs = (P("batch", "seq", None), P("batch", "seq", None), P("batch", None))
    out_specs = (P(("seq", "batch"), None), P(("seq", "batch"), None))
    return jax.shard_map(local, mesh=mesh, in_specs=in_specs, out_specs=out_specs, check_vma=False)
```

time: 128 us -> 38.1 us (0.30)
  waiting for transfers between devices: 89.2 us -> 0 us
  Pallas kernels: 0 us -> 35.5 us
  between operations: 14.1 us -> 0.64 us
  matrix products: 9.75 us -> 0 us
  local copies, waits for them, and re-layouts: 7.28 us -> 0.82 us
  starting transfers between devices: 4.83 us -> 0 us
  other arithmetic: 2.61 us -> 0.99 us
    all_gather x1 -> x0, waiting for transfers between devices: 83 us -> none  [sent_together(): whole = lax.all_gather(both, axis, axis=dim, tiled=True)]
    pallas_call x0 -> x1, Pallas kernels: none -> 35.5 us  [local(): pl.pallas_call(kernel, out_shape=jax.ShapeDtypeStruct((2, rows, width), B...]
    dot_general x4 -> x0, matrix products: 9.75 us -> none  [the longest x1 3.74 us: local(): act_part = jnp.dot(member, act_local, preferred_element_type=jnp.float32)]
    all_to_all x1 -> x0, waiting for transfers between devices: 6.23 us -> none  [copy_for_each(): lax.all_to_all(jnp.broadcast_to(value[None], (peers, *value.shape)), axis...]
    unnamed x3 -> x0, local copies, waits for them, and re-layouts: 5.99 us -> none
    all_to_all x1 -> x0, starting transfers between devices: 4.83 us -> none  [copy_for_each(): lax.all_to_all(jnp.broadcast_to(value[None], (peers, *value.shape)), axis...]
  transfers between devices with their start and end apart: 2 -> 0, of which waited for: 2 -> 0; matrix products, arithmetic and copies ran while one was open for 0% -> 0% of each run, Pallas kernels for 0% -> 0%
where the time goes in v1:
time: 38.1 us; the launch traced here: 38 us
  Pallas kernels  35.5 us (93%)
  other arithmetic  0.99 us (3%)
  local copies, waits for them, and re-layouts  0.82 us (2%)
  between operations  0.64 us (2%)
    pallas_call x1, Pallas kernels, local(): pl.pallas_call(kernel, out_shape=jax.ShapeDtypeStruct((2, rows, width), B...  35.5 us
    convert_element_type x1, other arithmetic, local(): wide_out = out.astype(F32)  0.99 us
    squeeze x1, local copies, waits for them, and re-layouts, local(): return (wide_out[0], wide_out[1])  0.82 us

profile of v1, /device:TPU:1, one launch (start us, length us, event | category | flops | bytes accessed | tf_op | source)
XLA Modules:
  0.0 38.0 jit_solution(5125284961348362879)
XLA Ops:
  0.6 35.5 %shard_map.50 = bf16[2,16,4096]{2,1,0:T(8,128)(2,1)} custom-call(bf16[1,768,4096]{2,1,0:T(8,128)(2,1)} %act_hbm.1, bf16[1,768,4096]{2,1,0:T(8,128)(2,1)} %grad_hbm.1, s32[1,3]{1,0:T(1,128)} %len_ref.1), custom_call_target="tpu_custom_call" | custom-call | tf_op jit(solution)/shard_map/pallas_call | solution.py:248
  36.2 1.0 %convert_element_type.3 = f32[2,16,4096]{2,1,0:T(8,128)S(1)} convert(bf16[2,16,4096]{2,1,0:T(8,128)(2,1)} %shard_map.50) | non-fusion elementwise | flops 131072 | bytes 786432 | tf_op jit(solution)/shard_map/convert_element_type | solution.py:276
  37.2 0.8 %slice_bitcast_fusion = (f32[16,4096]{1,0:T(8,128)}, f32[16,4096]{1,0:T(8,128)}) fusion(f32[2,16,4096]{2,1,0:T(8,128)S(1)} %convert_element_type.3), kind=kLoop, calls=%fused_computation | loop fusion | bytes 1048576 | tf_op jit(solution)/shard_map/squeeze | solution.py:277

commit v2 on v1

--- a/solution.py
+++ b/solution.py
@@ -98,8 +98,7 @@
     my_slot = x * NB + g_me
     home = x * NB + mine
 
-    @pl.loop(0, steps)
-    def _(i):
+    def sums(i):
         for copy in loads(i):
             copy.wait()
         total = jnp.dot(m_act, abuf[i], preferred_element_type=F32)
@@ -110,16 +109,30 @@
         for j in range(per_step):
             parts[first + j] = total[:, j * LANES : (j + 1) * LANES]
 
-        @pl.when(i == 0)
-        def _():
-            pl.semaphore_wait(barrier, NX * NB - 1 + NZ - 1 + NZ - jnp.where(mine == z, 1, 0))
-
+    def sends(i):
+        q = quarter(i)
+        first = q * NB + (i % halves) * per_step
         for j in range(per_step):
             zb = (i % halves) * per_step + j
 
             @pl.when(first + j != home)
             def _():
                 s1_copy(first + j, at(q, zb % NY, z, zb // NY), my_slot).start()
+
+    @pl.loop(0, 4)
+    def _(i):
+        sums(i)
+
+    pl.semaphore_wait(barrier, NX * NB - 1 + NZ - 1 + NZ - jnp.where(mine == z, 1, 0))
+
+    @pl.loop(0, 4)
+    def _(i):
+        sends(i)
+
+    @pl.loop(4, steps)
+    def _(i):
+        sums(i)
+        sends(i)
 
     got[my_slot] = parts[home]
     pltpu.make_async_copy(got.at[pl.ds(0, NX * NB - 1)], got.at[pl.ds(0, NX * NB - 1)], s1_recv).wait()
@@ -190,32 +203,27 @@
     grad_only = jnp.where(in_act, 0.0, 1.0).astype(BF16)
     both = jnp.concatenate([lcols * act_only, lcols * grad_only], axis=1)
 
-    for k in range(1, NX):
+    for k in (0, 1, 3, 2):
         who = (x + k) % NX
-        arrived(rhs.at[who], x_recv.at[who])
-
-    for k in range(NX):
+        if k:
+            arrived(rhs.at[who], x_recv.at[who])
         product = lax.dot_general(
-            both, rhs[k].reshape(depth, LANES), (((0,), (0,)), ((), ())), preferred_element_type=F32
+            both, rhs[who].reshape(depth, LANES), (((0,), (0,)), ((), ())), preferred_element_type=F32
         )
         product = (product / total_seqs).astype(BF16)
         for d in range(NB):
             for kind in range(2):
-                tiles[d, kind * rows : (kind + 1) * rows, k * LANES : (k + 1) * LANES] = product[
+                tiles[k, d, kind * rows : (kind + 1) * rows] = product[
                     kind * LANES + d * rows : kind * LANES + (d + 1) * rows
                 ]
-
-    def o_copy(d):
-        return pltpu.make_async_remote_copy(
-            src_ref=tiles.at[d], dst_ref=landed.at[mine],
-            send_sem=o_send, recv_sem=o_recv,
-            device_id=at(x, d // NC, z, d % NC), device_id_type=MESH,
-        )
-
-    for k in (4, 5, 2, 3, 6, 7, 1):
-        d = (g_me + k) % NB
-        o_copy(d).start()
-    landed[mine] = tiles[g_me]
+        for step in (4, 5, 2, 3, 6, 7, 1):
+            d = (g_me + step) % NB
+            pltpu.make_async_remote_copy(
+                src_ref=tiles.at[k, d], dst_ref=landed.at[who, mine],
+                send_sem=o_send.at[k], recv_sem=o_recv.at[who],
+                device_id=at(x, d // NC, z, d % NC), device_id_type=MESH,
+            ).start()
+        landed[who, mine] = tiles[k, g_me]
 
     arrived(got.at[pl.ds(0, NX * NB - 1)], s1_send)
     arrived(rhs.at[0, pl.ds(0, NZ - 1)], z_send)
@@ -229,13 +237,15 @@
     def _():
         arrived(lhs.at[pl.ds(0, NB)], l_send)
 
-    arrived(landed.at[pl.ds(0, NB - 1)], o_recv)
-    arrived(landed.at[pl.ds(0, NB - 1)], o_send)
+    for k in range(NX):
+        arrived(landed.at[k, pl.ds(0, NB - 1)], o_send.at[k])
+    for q in range(NX):
+        arrived(landed.at[q, pl.ds(0, NB - 1)], o_recv.at[q])
     for q in range(NX):
         for zb in range(NB):
             cols = pl.ds((q * NB + zb) * LANES, LANES)
             for kind in range(2):
-                out_ref[kind, :, cols] = landed[zb, kind * rows : (kind + 1) * rows, q * LANES : (q + 1) * LANES]
+                out_ref[kind, :, cols] = landed[q, zb, kind * rows : (kind + 1) * rows]
 
 
 def local(activations, out_grads, lengths):
@@ -247,7 +257,7 @@
     dma = pltpu.SemaphoreType.DMA
     out = pl.pallas_call(
         kernel,
-        out_shape=jax.ShapeDtypeStruct((2, rows, width), BF16),
+        out_shape=pltpu.VMEM((2, rows, width), BF16),
         in_specs=[
             pl.BlockSpec(memory_space=pl.ANY),
             pl.BlockSpec(memory_space=pl.ANY),
@@ -262,19 +272,18 @@
             pltpu.VMEM((chunk, LANES), F32),
             pltpu.VMEM((NX, NZ, chunk, LANES), BF16),
             pltpu.VMEM((NZ, chunk, LANES), BF16),
-            pltpu.VMEM((NB, 2 * rows, NX * LANES), BF16),
-            pltpu.VMEM((NB, 2 * rows, NX * LANES), BF16),
+            pltpu.VMEM((NX, NB, 2 * rows, LANES), BF16),
+            pltpu.VMEM((NX, NB, 2 * rows, LANES), BF16),
             dma((2, steps)),
             dma, dma,
             dma, dma((NZ,)),
             dma, dma((NX,)),
             dma, dma((NZ,)),
-            dma, dma,
+            dma((NX,)), dma((NX,)),
         ],
         compiler_params=pltpu.CompilerParams(collective_id=0, has_side_effects=True),
     )(activations, out_grads, lengths)
-    wide_out = out.astype(F32)
-    return wide_out[0], wide_out[1]
+    return out[0].astype(F32), out[1].astype(F32)
 
 
 def solution(mesh):

time: 38.1 us -> 35 us (0.919)
  Pallas kernels: 35.5 us -> 33.5 us
  local copies, waits for them, and re-layouts: 0.82 us -> 0 us
    pallas_call x1, Pallas kernels: 35.5 us -> 33.5 us  [local(): pl.pallas_call(kernel, out_shape=pltpu.VMEM((2, rows, width), BF16), in_s...]
    squeeze x1 -> x0, local copies, waits for them, and re-layouts: 0.82 us -> none  [local(): return (wide_out[0], wide_out[1])]
where the time goes in v2:
time: 35 us; the launch traced here: 34.9 us
  Pallas kernels  33.5 us (96%)
  other arithmetic  0.83 us (2%)
  between operations  0.64 us (2%)
    pallas_call x1, Pallas kernels, local(): pl.pallas_call(kernel, out_shape=pltpu.VMEM((2, rows, width), BF16), in_s...  33.5 us
    convert_element_type x1, other arithmetic, local(): return (out[0].astype(F32), out[1].astype(F32))  0.83 us

profile of v2, /device:TPU:1, one launch (start us, length us, event | category | flops | bytes accessed | tf_op | source)
XLA Modules:
  0.0 34.9 jit_solution(15201361938938956468)
XLA Ops:
  0.6 33.5 %shard_map.50 = bf16[2,16,4096]{2,1,0:T(8,128)(2,1)S(1)} custom-call(bf16[1,768,4096]{2,1,0:T(8,128)(2,1)} %act_hbm.1, bf16[1,768,4096]{2,1,0:T(8,128)(2,1)} %grad_hbm.1, s32[1,3]{1,0:T(1,128)} %len_ref.1), custom_call_target="tpu_custom_call" | custom-call | tf_op jit(solution)/shard_map/pallas_call | solution.py:258
  34.1 0.8 %bitcast_convert_fusion = (f32[16,4096]{1,0:T(8,128)}, f32[16,4096]{1,0:T(8,128)}) fusion(bf16[2,16,4096]{2,1,0:T(8,128)(2,1)S(1)} %shard_map.50), kind=kLoop, calls=%fused_computation | loop fusion | flops 131072 | bytes 786432 | tf_op jit(solution)/shard_map/convert_element_type | solution.py:286

commit v3 on v2

--- a/solution.py
+++ b/solution.py
@@ -9,6 +9,7 @@
 NB = NY * NC
 LANES = 128
 SEQS = 3
+HELD = 4
 MESH = pl.DeviceIdType.MESH
 F32, BF16 = jnp.float32, jnp.bfloat16
 
@@ -16,7 +17,7 @@
 def kernel(
     act_hbm, grad_hbm, len_ref, out_ref,
     abuf, gbuf, parts, got, packed, rhs, lhs, tiles, landed,
-    in_sem, s1_send, s1_recv, z_send, z_recv, x_send, x_recv, l_send, l_recv, o_send, o_recv,
+    in_sem, s1_send, s1_recv, z_send, z_recv, x_send, x_recv, l_send, l_recv, d_send, o_send, o_recv,
 ):
     steps, tokens, wide = abuf.shape
     halves = steps // NX
@@ -56,23 +57,24 @@
     def greet(target):
         pl.semaphore_signal(barrier, inc=1, device_id=target, device_id_type=MESH)
 
-    @pl.loop(1, NX * NB)
-    def _(k):
-        other = (x * NB + g_me + k) % (NX * NB)
-        greet(at(other // NB, (other % NB) // NC, z, other % NC))
-
-    @pl.loop(1, NZ)
-    def _(k):
-        greet(at(x, y, (z + k) % NZ, c))
-
     src_y, src_c = z % NY, z // NY
     src_here = jnp.logical_and(src_y == y, src_c == c)
 
-    @pl.loop(0, NZ)
-    def _(k):
-        @pl.when(jnp.logical_not(jnp.logical_and(src_here, k == z)))
+    for k in (4, 3, 5, 2, 6, 1, 7, 0):
+        layer = (z + k) % NZ
+
+        if k:
+            greet(at(x, y, layer, c))
+
+        @pl.when((layer % NC == c) & jnp.logical_not(src_here & (layer == z)))
         def _():
-            greet(at(x, src_y, k, src_c))
+            greet(at(x, src_y, layer, src_c))
+
+    for dx in (2, 1, 3, 0):
+        for dy in (2, 1, 3, 0):
+            for dc in range(NC):
+                if dx or dy or dc:
+                    greet(at((x + dx) % NX, (y + dy) % NY, z, (c + dc) % NC))
 
     l0, l1, l2 = len_ref[0, 0], len_ref[0, 1], len_ref[0, 2]
     row = lax.broadcasted_iota(jnp.int32, (8, tokens), 0)
@@ -119,18 +121,16 @@
             def _():
                 s1_copy(first + j, at(q, zb % NY, z, zb // NY), my_slot).start()
 
-    @pl.loop(0, 4)
-    def _(i):
+    for i in range(HELD):
         sums(i)
 
-    pl.semaphore_wait(barrier, NX * NB - 1 + NZ - 1 + NZ - jnp.where(mine == z, 1, 0))
-
-    @pl.loop(0, 4)
+    pl.semaphore_wait(barrier, NX * NB - 1 + NZ - 1 + NY - jnp.where((mine == z) & (z % NC == c), 1, 0))
+
+    @pl.loop(0, HELD)
     def _(i):
         sends(i)
 
-    @pl.loop(4, steps)
-    def _(i):
+    for i in range(HELD, steps):
         sums(i)
         sends(i)
 
@@ -146,7 +146,7 @@
     own = packed[...].astype(BF16)
     rhs[x, z] = own
 
-    @pl.when(mine == z)
+    @pl.when((mine == z) & (z % NC == c))
     def _():
         lhs[z] = own
 
@@ -175,12 +175,12 @@
         z_copy(k).start()
     for k in (2, 1, 3):
         x_copy(k, z).start()
-    for k in range(NB):
-        d = (g_me + 4 + k) % NB
-
-        @pl.when(jnp.logical_not(jnp.logical_and(mine == z, d == g_me)))
+    for k in (2, 1, 3, 0):
+        to_y = (y + k) % NY
+
+        @pl.when(jnp.logical_not((mine == z) & (z % NC == c) & (to_y == y)))
         def _():
-            l_copy(d).start()
+            l_copy(to_y * NC + z % NC).start()
 
     def arrived(ref, sem):
         pltpu.make_async_copy(ref, ref, sem).wait()
@@ -191,24 +191,38 @@
         for kx in (2, 1, 3):
             x_copy(kx, layer).start()
 
-    for k in range(NZ):
-        @pl.when(jnp.logical_not(jnp.logical_and(src_here, k == z)))
+    def hand_over(layer):
+        return pltpu.make_async_remote_copy(
+            src_ref=lhs.at[layer], dst_ref=lhs.at[layer],
+            send_sem=d_send, recv_sem=l_recv.at[layer],
+            device_id=at(x, y, z, 1 - c), device_id_type=MESH,
+        )
+
+    for k in range(NZ // NC):
+        layer = (z + c + z % NC + (0, 6, 2, 4)[k]) % NZ
+
+        @pl.when(jnp.logical_not(src_here & (layer == z)))
         def _():
-            arrived(lhs.at[k], l_recv.at[k])
+            arrived(lhs.at[layer], l_recv.at[layer])
+
+        hand_over(layer).start()
+    for k in range(NZ // NC):
+        layer = NC * k + 1 - c
+        arrived(lhs.at[layer], l_recv.at[layer])
 
     depth = NZ * chunk
     lcols = lhs[...].reshape(depth, LANES)
     in_act = lax.broadcasted_iota(jnp.int32, (depth, LANES), 0) % chunk < SEQS * NB
     act_only = jnp.where(in_act, 1.0, 0.0).astype(BF16)
     grad_only = jnp.where(in_act, 0.0, 1.0).astype(BF16)
-    both = jnp.concatenate([lcols * act_only, lcols * grad_only], axis=1)
+    both = jnp.concatenate([lcols * act_only, lcols * grad_only], axis=1).T
 
     for k in (0, 1, 3, 2):
         who = (x + k) % NX
         if k:
             arrived(rhs.at[who], x_recv.at[who])
         product = lax.dot_general(
-            both, rhs[who].reshape(depth, LANES), (((0,), (0,)), ((), ())), preferred_element_type=F32
+            both, rhs[who].reshape(depth, LANES), (((1,), (0,)), ((), ())), preferred_element_type=F32
         )
         product = (product / total_seqs).astype(BF16)
         for d in range(NB):
@@ -229,14 +243,17 @@
     arrived(rhs.at[0, pl.ds(0, NZ - 1)], z_send)
     arrived(rhs.at[pl.ds(0, NX - 1)], x_send)
 
-    @pl.when(mine == z)
+    alone = (mine == z) & (z % NC == c)
+
+    @pl.when(alone)
     def _():
-        arrived(lhs.at[pl.ds(0, NB - 1)], l_send)
-
-    @pl.when(mine != z)
+        arrived(lhs.at[pl.ds(0, NY - 1)], l_send)
+
+    @pl.when(jnp.logical_not(alone))
     def _():
-        arrived(lhs.at[pl.ds(0, NB)], l_send)
-
+        arrived(lhs.at[pl.ds(0, NY)], l_send)
+
+    arrived(lhs.at[pl.ds(0, NZ // NC)], d_send)
     for k in range(NX):
         arrived(landed.at[k, pl.ds(0, NB - 1)], o_send.at[k])
     for q in range(NX):
@@ -278,7 +295,7 @@
             dma, dma,
             dma, dma((NZ,)),
             dma, dma((NX,)),
-            dma, dma((NZ,)),
+            dma, dma((NZ,)), dma,
             dma((NX,)), dma((NX,)),
         ],
         compiler_params=pltpu.CompilerParams(collective_id=0, has_side_effects=True),

time: 35 us -> 33 us (0.943)
  Pallas kernels: 33.5 us -> 31.4 us
    pallas_call x1, Pallas kernels: 33.5 us -> 31.4 us  [local(): pl.pallas_call(kernel, out_shape=pltpu.VMEM((2, rows, width), BF16), in_s...]
where the time goes in v3:
time: 33 us; the launch traced here: 32.9 us
  Pallas kernels  31.4 us (95%)
  other arithmetic  0.83 us (3%)
  between operations  0.64 us (2%)
    pallas_call x1, Pallas kernels, local(): pl.pallas_call(kernel, out_shape=pltpu.VMEM((2, rows, width), BF16), in_s...  31.4 us
    convert_element_type x1, other arithmetic, local(): return (out[0].astype(F32), out[1].astype(F32))  0.83 us

profile of v3, /device:TPU:1, one launch (start us, length us, event | category | flops | bytes accessed | tf_op | source)
XLA Modules:
  0.0 32.9 jit_solution(204087944933402862)
XLA Ops:
  0.6 31.4 %shard_map.50 = bf16[2,16,4096]{2,1,0:T(8,128)(2,1)S(1)} custom-call(bf16[1,768,4096]{2,1,0:T(8,128)(2,1)} %act_hbm.1, bf16[1,768,4096]{2,1,0:T(8,128)(2,1)} %grad_hbm.1, s32[1,3]{1,0:T(1,128)} %len_ref.1), custom_call_target="tpu_custom_call" | custom-call | tf_op jit(solution)/shard_map/pallas_call | solution.py:275
  32.1 0.8 %bitcast_convert_fusion = (f32[16,4096]{1,0:T(8,128)}, f32[16,4096]{1,0:T(8,128)}) fusion(bf16[2,16,4096]{2,1,0:T(8,128)(2,1)S(1)} %shard_map.50), kind=kLoop, calls=%fused_computation | loop fusion | flops 131072 | bytes 786432 | tf_op jit(solution)/shard_map/convert_element_type | solution.py:303

commit v4 on v3

--- a/solution.py
+++ b/solution.py
@@ -37,18 +37,33 @@
     def at(x_, y_, z_, c_):
         return (x_, (z_ * NY + y_) * NC + c_)
 
-    def quarter(i):
-        return (x + 1 + i // halves) % NX
+    whole = steps - steps // NX
+    pieces = 2 * steps // NX
+    span = per_step // 2
+
+    def blocks(i):
+        if i < whole:
+            return (x + 1 + i // halves) % NX, (i % halves) * per_step, per_step
+        p = i - whole
+        pair = y // span if p >= halves else 1 - y // span
+        return x, (p % halves) * per_step + pair * span, span
+
+    def views(i):
+        if i < whole:
+            return abuf.at[i], gbuf.at[i]
+        slot, half = whole + (i - whole) // 2, pl.ds((i - whole) % 2 * span * LANES, span * LANES)
+        return abuf.at[slot, :, half], gbuf.at[slot, :, half]
 
     def loads(i):
-        cols = pl.ds(pl.multiple_of(quarter(i) * (halves * wide) + (i % halves) * wide, wide), wide)
+        q, first, count = blocks(i)
+        cols = pl.ds(pl.multiple_of((q * NB + first) * LANES, span * LANES), count * LANES)
+        a_view, g_view = views(i)
         return (
-            pltpu.make_async_copy(act_hbm.at[0, :, cols], abuf.at[i], in_sem.at[0, i]),
-            pltpu.make_async_copy(grad_hbm.at[0, :, cols], gbuf.at[i], in_sem.at[1, i]),
-        )
-
-    @pl.loop(0, steps)
-    def _(i):
+            pltpu.make_async_copy(act_hbm.at[0, :, cols], a_view, in_sem.at[0, i]),
+            pltpu.make_async_copy(grad_hbm.at[0, :, cols], g_view, in_sem.at[1, i]),
+        )
+
+    for i in range(whole + pieces):
         for copy in loads(i):
             copy.start()
 
@@ -93,7 +108,7 @@
 
     def s1_copy(slot_block, target, slot):
         return pltpu.make_async_remote_copy(
-            src_ref=parts.at[slot_block], dst_ref=got.at[slot],
+            src_ref=parts.at[slot_block, pl.ds(0, 2 * SEQS)], dst_ref=got.at[slot, pl.ds(0, 2 * SEQS)],
             send_sem=s1_send, recv_sem=s1_recv, device_id=target, device_id_type=MESH,
         )
 
@@ -103,39 +118,37 @@
     def sums(i):
         for copy in loads(i):
             copy.wait()
-        total = jnp.dot(m_act, abuf[i], preferred_element_type=F32)
-        total += jnp.dot(m_grad, gbuf[i], preferred_element_type=F32)
-        total = total / divisor
-        q = quarter(i)
-        first = q * NB + (i % halves) * per_step
-        for j in range(per_step):
-            parts[first + j] = total[:, j * LANES : (j + 1) * LANES]
+        q, first, count = blocks(i)
+        a_view, g_view = views(i)
+        total = jnp.dot(m_act, a_view[...], preferred_element_type=F32)
+        total += jnp.dot(m_grad, g_view[...], preferred_element_type=F32)
+        total = total / divisor[:, : count * LANES]
+        for j in range(count):
+            parts[q * NB + first + j] = total[:, j * LANES : (j + 1) * LANES]
 
     def sends(i):
-        q = quarter(i)
-        first = q * NB + (i % halves) * per_step
-        for j in range(per_step):
-            zb = (i % halves) * per_step + j
-
-            @pl.when(first + j != home)
+        q, first, count = blocks(i)
+        for j in range(count):
+            zb = first + j
+
+            @pl.when(q * NB + zb != home)
             def _():
-                s1_copy(first + j, at(q, zb % NY, z, zb // NY), my_slot).start()
+                s1_copy(q * NB + zb, at(q, zb % NY, z, zb // NY), my_slot).start()
 
     for i in range(HELD):
         sums(i)
 
     pl.semaphore_wait(barrier, NX * NB - 1 + NZ - 1 + NY - jnp.where((mine == z) & (z % NC == c), 1, 0))
 
-    @pl.loop(0, HELD)
-    def _(i):
+    for i in range(HELD):
         sends(i)
 
-    for i in range(HELD, steps):
+    for i in range(HELD, whole + pieces):
         sums(i)
         sends(i)
 
     got[my_slot] = parts[home]
-    pltpu.make_async_copy(got.at[pl.ds(0, NX * NB - 1)], got.at[pl.ds(0, NX * NB - 1)], s1_recv).wait()
+    pltpu.make_async_copy(got.at[pl.ds(0, NX * NB - 1), pl.ds(0, 2 * SEQS)], got.at[pl.ds(0, NX * NB - 1), pl.ds(0, 2 * SEQS)], s1_recv).wait()
 
     for g in range(NB):
         summed = got[g]
@@ -239,7 +252,7 @@
             ).start()
         landed[who, mine] = tiles[k, g_me]
 
-    arrived(got.at[pl.ds(0, NX * NB - 1)], s1_send)
+    arrived(got.at[pl.ds(0, NX * NB - 1), pl.ds(0, 2 * SEQS)], s1_send)
     arrived(rhs.at[0, pl.ds(0, NZ - 1)], z_send)
     arrived(rhs.at[pl.ds(0, NX - 1)], x_send)
 
@@ -291,7 +304,7 @@
             pltpu.VMEM((NZ, chunk, LANES), BF16),
             pltpu.VMEM((NX, NB, 2 * rows, LANES), BF16),
             pltpu.VMEM((NX, NB, 2 * rows, LANES), BF16),
-            dma((2, steps)),
+            dma((2, steps + steps // NX)),
             dma, dma,
             dma, dma((NZ,)),
             dma, dma((NX,)),

time: 33 us -> 32.9 us (level)
  no operation moved by 1% of the time
where the time goes in v4:
time: 32.9 us; the launch traced here: 32.8 us
  Pallas kernels  31.3 us (95%)
  other arithmetic  0.83 us (3%)
  between operations  0.64 us (2%)
    pallas_call x1, Pallas kernels, local(): pl.pallas_call(kernel, out_shape=pltpu.VMEM((2, rows, width), BF16), in_s...  31.3 us
    convert_element_type x1, other arithmetic, local(): return (out[0].astype(F32), out[1].astype(F32))  0.83 us

profile of v4, /device:TPU:1, one launch (start us, length us, event | category | flops | bytes accessed | tf_op | source)
XLA Modules:
  0.0 32.8 jit_solution(14215926325215585944)
XLA Ops:
  0.6 31.3 %shard_map.50 = bf16[2,16,4096]{2,1,0:T(8,128)(2,1)S(1)} custom-call(bf16[1,768,4096]{2,1,0:T(8,128)(2,1)} %act_hbm.1, bf16[1,768,4096]{2,1,0:T(8,128)(2,1)} %grad_hbm.1, s32[1,3]{1,0:T(1,128)} %len_ref.1), custom_call_target="tpu_custom_call" | custom-call | tf_op jit(solution)/shard_map/pallas_call | solution.py:288
  31.9 0.8 %bitcast_convert_fusion = (f32[16,4096]{1,0:T(8,128)}, f32[16,4096]{1,0:T(8,128)}) fusion(bf16[2,16,4096]{2,1,0:T(8,128)(2,1)S(1)} %shard_map.50), kind=kLoop, calls=%fused_computation | loop fusion | flops 131072 | bytes 786432 | tf_op jit(solution)/shard_map/convert_element_type | solution.py:316

commit v5 on v4

--- a/solution.py
+++ b/solution.py
@@ -252,6 +252,14 @@
             ).start()
         landed[who, mine] = tiles[k, g_me]
 
+    for k in (0, 1, 3, 2):
+        who = (x + k) % NX
+        arrived(landed.at[who, pl.ds(0, NB - 1)], o_recv.at[who])
+        for zb in range(NB):
+            cols = pl.ds(pl.multiple_of((who * NB + zb) * LANES, LANES), LANES)
+            for kind in range(2):
+                out_ref[kind, :, cols] = landed[who, zb, kind * rows : (kind + 1) * rows]
+
     arrived(got.at[pl.ds(0, NX * NB - 1), pl.ds(0, 2 * SEQS)], s1_send)
     arrived(rhs.at[0, pl.ds(0, NZ - 1)], z_send)
     arrived(rhs.at[pl.ds(0, NX - 1)], x_send)
@@ -269,13 +277,6 @@
     arrived(lhs.at[pl.ds(0, NZ // NC)], d_send)
     for k in range(NX):
         arrived(landed.at[k, pl.ds(0, NB - 1)], o_send.at[k])
-    for q in range(NX):
-        arrived(landed.at[q, pl.ds(0, NB - 1)], o_recv.at[q])
-    for q in range(NX):
-        for zb in range(NB):
-            cols = pl.ds((q * NB + zb) * LANES, LANES)
-            for kind in range(2):
-                out_ref[kind, :, cols] = landed[q, zb, kind * rows : (kind + 1) * rows]
 
 
 def local(activations, out_grads, lengths):

time: 32.9 us -> 32.8 us (level)
  no operation moved by 1% of the time
where the time goes in v5:
time: 32.8 us; the launch traced here: 32.7 us
  Pallas kernels  31.3 us (95%)
  other arithmetic  0.83 us (3%)
  between operations  0.64 us (2%)
    pallas_call x1, Pallas kernels, local(): pl.pallas_call(kernel, out_shape=pltpu.VMEM((2, rows, width), BF16), in_s...  31.3 us
    convert_element_type x1, other arithmetic, local(): return (out[0].astype(F32), out[1].astype(F32))  0.83 us

profile of v5, /device:TPU:1, one launch (start us, length us, event | category | flops | bytes accessed | tf_op | source)
XLA Modules:
  0.0 32.7 jit_solution(9314648624525240104)
XLA Ops:
  0.6 31.3 %shard_map.50 = bf16[2,16,4096]{2,1,0:T(8,128)(2,1)S(1)} custom-call(bf16[1,768,4096]{2,1,0:T(8,128)(2,1)} %act_hbm.1, bf16[1,768,4096]{2,1,0:T(8,128)(2,1)} %grad_hbm.1, s32[1,3]{1,0:T(1,128)} %len_ref.1), custom_call_target="tpu_custom_call" | custom-call | tf_op jit(solution)/shard_map/pallas_call | solution.py:289
  31.9 0.8 %bitcast_convert_fusion = (f32[16,4096]{1,0:T(8,128)}, f32[16,4096]{1,0:T(8,128)}) fusion(bf16[2,16,4096]{2,1,0:T(8,128)(2,1)S(1)} %shard_map.50), kind=kLoop, calls=%fused_computation | loop fusion | flops 131072 | bytes 786432 | tf_op jit(solution)/shard_map/convert_element_type | solution.py:317
